TPU v7x, 32 devices: a whole 2x2x4 slice. The times are simulated.
32 devices in a mesh: dp: 8 (over z, y), mp: 4 (over x, core).
Axes of the slice: x: 2, y: 2, z: 4, core: 2. Of those that a mesh axis runs over, the one named last changes fastest.
Arguments:
- tokens: bfloat16 [49152, 512], P('dp'), may hold values from -6 to 6
- w_uvqk: bfloat16 [512, 2048], P(None, 'mp')
- w_out: bfloat16 [512, 512], replicated, may hold values from -0.25 to 0.25
- hist_len: int32 [8, 24], P('dp'), may hold values from 64 to 256, as said below
- owner: int32 [8, 24], P('dp'), may hold values from 0 to 7, as said below
- recv_offset: int32 [8, 24], P('dp'), may hold values from 0 to 47, as said below
- block_start: int32 [8, 24], P('dp'), may hold values from 0 to 47, as said below
Outputs:
- packed_out: bfloat16 [49152, 512], P('dp', 'mp')
- user_state: bfloat16 [192, 512], P('dp', 'mp')
Inputs may be any that keep to these rules, and one draw needn't show every extreme that they name: User (d, u) has ceil(hist_len / 128) blocks, at most 2. owner[d, u] = (p(d) + r(u mod 8)) mod 8 for two permutations p, r of the indices of dp drawn from the seed: every owner receives exactly 24 users, and one device sends at most 3 users to one owner. On some owner every received user has 2 blocks. `recv_offset`: the users of one owner occupy disjoint runs of its 48 blocks, in the order of u; on some owner they fill all 48 blocks. `block_start`: the users of one device occupy disjoint runs of its 48 blocks, in the order of u.
All inputs are finite; a program needn't handle non-finite values.
Results may differ from a plain program's by a relative error of at most 0.0059.
Values may be sent and summed in bfloat16 or wider, within the bound.
A program may use at most 128 MiB of HBM per device.

v0:
```python
import jax
import jax.numpy as jnp
from jax import lax
from jax.sharding import PartitionSpec as P

D = 512
HEADS = 4
BLOCK = 128
MAXB = 2
BLK_DEV = 48
EPS = 1e-05


def norm_rows(values):
    average = jnp.mean(values, axis=-1, keepdims=True)
    variance = jnp.mean(values * values, axis=-1, keepdims=True) - average * average
    return (values - average) * lax.rsqrt(variance + EPS)


def attend(query, keys, values, query_user, key_user):
    row_count, head_size = query.shape
    tile_rows = 4 * BLOCK
    back_rows = (MAXB - 1) * BLOCK
    scaling = (D // HEADS) ** (-0.5)
    keys_ext = jnp.concatenate([jnp.zeros((back_rows, head_size), keys.dtype), keys], 0)
    values_ext = jnp.concatenate([jnp.zeros((back_rows, head_size), values.dtype), values], 0)
    users_ext = jnp.concatenate([jnp.full((back_rows,), -2, jnp.int32), key_user], 0)
    query_pos = jnp.arange(tile_rows, dtype=jnp.int32)[:, None] + back_rows
    key_pos = jnp.arange(tile_rows + back_rows, dtype=jnp.int32)[None, :]

    def one_tile(start):
        query_tile = lax.dynamic_slice_in_dim(query, start, tile_rows, 0)
        key_tile = lax.dynamic_slice_in_dim(keys_ext, start, tile_rows + back_rows, 0)
        value_tile = lax.dynamic_slice_in_dim(values_ext, start, tile_rows + back_rows, 0)
        query_owner = lax.dynamic_slice_in_dim(query_user, start, tile_rows, 0)
        key_owner = lax.dynamic_slice_in_dim(users_ext, start, tile_rows + back_rows, 0)
        raw_scores = (
            lax.dot_general(
                query_tile, key_tile, (((1,), (1,)), ((), ())), preferred_element_type=jnp.float32
            )
            * scaling
        )
        allowed = (query_owner[:, None] == key_owner[None, :]) & (key_pos <= query_pos)
        weights = jnp.where(allowed, jax.nn.silu(raw_scores) / (MAXB * BLOCK), 0.0).astype(
            jnp.bfloat16
        )
        return jnp.dot(weights, value_tile, preferred_element_type=jnp.float32)

    tile_starts = jnp.arange(row_count // tile_rows, dtype=jnp.int32) * tile_rows
    return lax.map(one_tile, tile_starts).reshape(row_count, head_size)


def layer_rows(rows_in, query_user, key_user, w_uvqk, w_out):
    row_count = rows_in.shape[0]
    head_size = D // HEADS
    mp_size = lax.axis_size("mp")
    portion = lax.axis_index("mp")
    quarter = D // mp_size
    local_heads = w_uvqk.shape[1] // (4 * head_size)
    widened = rows_in.astype(jnp.float32)
    normed = norm_rows(widened).astype(jnp.bfloat16)
    projected = jax.nn.silu(jnp.dot(normed, w_uvqk, preferred_element_type=jnp.float32)).astype(
        jnp.bfloat16
    )
    pieces = projected.reshape(row_count, local_heads, 4, head_size)
    outputs = attend(pieces[:, 0, 2], pieces[:, 0, 3], pieces[:, 0, 1], query_user, key_user)
    totals = lax.psum((jnp.sum(outputs, 1), jnp.sum(outputs * outputs, 1)), "mp")
    average = totals[0] / D
    variance = totals[1] / D - average * average
    gates = pieces[:, :, 0].reshape(row_count, local_heads * head_size).astype(jnp.float32)
    gated_rows = ((outputs - average[:, None]) * lax.rsqrt(variance + EPS)[:, None] * gates).astype(
        jnp.bfloat16
    )
    own_rows = lax.dynamic_slice_in_dim(
        w_out, portion * local_heads * head_size, local_heads * head_size, 0
    )
    partial_term = jnp.dot(gated_rows, own_rows, preferred_element_type=jnp.float32)
    mixed_rows = lax.psum_scatter(partial_term, "mp", scatter_dimension=1, tiled=True)
    residual = lax.dynamic_slice_in_dim(widened, portion * quarter, quarter, 1)
    return (mixed_rows + residual).astype(jnp.bfloat16)


def row_labels(block_user, block_fill):
    in_block = jnp.arange(BLOCK, dtype=jnp.int32)[None, :]
    row_live = (in_block < block_fill[:, None]).reshape(-1)
    row_user = jnp.broadcast_to(block_user[:, None], (block_user.shape[0], BLOCK)).reshape(-1)
    return (row_live, jnp.where(row_live, row_user, -3), jnp.where(row_live, row_user, -2))


def per_device(tokens, w_uvqk, w_out, hist_len, owner, recv_offset, block_start):
    dp_size = lax.axis_size("dp")
    mp_size = lax.axis_size("mp")
    myself = lax.axis_index("dp")
    user_count = hist_len.shape[1]
    per_pair = -(-user_count // dp_size)
    pair_cap = per_pair * MAXB
    quarter = D // mp_size
    lengths = hist_len[0]
    owners = owner[0]
    starts = block_start[0]
    counts = (lengths + BLOCK - 1) // BLOCK
    user_ids = jnp.arange(user_count, dtype=jnp.int32)
    earlier = user_ids[None, :] < user_ids[:, None]
    same_owner = (owners[:, None] == owners[None, :]) & earlier
    in_pair = jnp.sum(jnp.where(same_owner, counts[None, :], 0), axis=1)
    slot_ids = jnp.arange(pair_cap, dtype=jnp.int32)
    device_ids = jnp.arange(dp_size, dtype=jnp.int32)
    slot_step = slot_ids[None, :, None] - in_pair[None, None, :]
    sending = (
        (owners[None, None, :] == device_ids[:, None, None])
        & (slot_step >= 0)
        & (slot_step < counts[None, None, :])
    )
    send_block = jnp.sum(jnp.where(sending, starts[None, None, :] + slot_step, 0), axis=2)
    all_len, all_owner, all_offset = (
        lax.all_gather(hist_len, "dp", axis=0, tiled=True),
        lax.all_gather(owner, "dp", axis=0, tiled=True),
        lax.all_gather(recv_offset, "dp", axis=0, tiled=True),
    )
    all_counts = (all_len + BLOCK - 1) // BLOCK
    all_before = (all_owner[:, :, None] == all_owner[:, None, :]) & earlier[None]
    all_in_pair = jnp.sum(jnp.where(all_before, all_counts[:, None, :], 0), axis=2)
    owned = all_owner == myself
    flat_owned = owned.reshape(-1)
    flat_len = all_len.reshape(-1)
    flat_offset = all_offset.reshape(-1)
    flat_counts = all_counts.reshape(-1)
    flat_in_pair = all_in_pair.reshape(-1)
    candidate_ids = jnp.arange(dp_size * user_count, dtype=jnp.int32)
    source_ids = candidate_ids // user_count
    block_ids = jnp.arange(BLK_DEV, dtype=jnp.int32)
    land_step = block_ids[:, None] - flat_offset[None, :]
    landed = flat_owned[None, :] & (land_step >= 0) & (land_step < flat_counts[None, :])
    slot_index = jnp.sum(
        jnp.where(landed, source_ids[None, :] * pair_cap + flat_in_pair[None, :] + land_step, 0),
        axis=1,
    )
    owned_user = jnp.sum(jnp.where(landed, candidate_ids[None, :], 0), axis=1)
    owned_fill = jnp.sum(
        jnp.where(landed, jnp.clip(flat_len[None, :] - land_step * BLOCK, 0, BLOCK), 0), axis=1
    )
    owned_live, owned_query, owned_key = row_labels(owned_user, owned_fill)
    local_step = block_ids[:, None] - starts[None, :]
    within = (local_step >= 0) & (local_step < counts[None, :])
    local_user = jnp.sum(jnp.where(within, user_ids[None, :], 0), axis=1)
    local_fill = jnp.sum(
        jnp.where(within, jnp.clip(lengths[None, :] - local_step * BLOCK, 0, BLOCK), 0), axis=1
    )
    local_live, local_query, local_key = row_labels(local_user, local_fill)
    results = layer_rows(tokens, local_query, local_key, w_uvqk, w_out)
    state = jnp.take(results, starts * BLOCK + lengths - 1, axis=0)
    outgoing = jnp.take(results.reshape(BLK_DEV, BLOCK, quarter), send_block, axis=0)
    arrived = lax.all_to_all(outgoing, "dp", split_axis=0, concat_axis=0, tiled=True)
    gathered = jnp.take(
        arrived.reshape(dp_size * pair_cap, BLOCK, quarter), slot_index, axis=0
    ).reshape(BLK_DEV * BLOCK, quarter)
    packed = jnp.where(owned_live[:, None], gathered, jnp.zeros_like(gathered))
    return (packed, state)


def solution(mesh):
    in_specs = (
        P("dp", None),
        P(None, "mp"),
        P(),
        P("dp", None),
        P("dp", None),
        P("dp", None),
        P("dp", None),
    )
    out_specs = (P("dp", "mp"), P("dp", "mp"))
    return jax.shard_map(
        per_device, mesh=mesh, in_specs=in_specs, out_specs=out_specs, check_vma=False
    )
```

profile of v0, /device:TPU:0, one launch (start us, length us, event | category | flops | bytes accessed | tf_op | source)
XLA Modules:
  0.0 330.3 jit_solution(3480145487422922043)
XLA Ops:
  7.3 4.8 %convert_reduce_fusion = (f32[6144]{0:T(1024)S(1)}, f32[6144]{0:T(1024)S(1)}) fusion(bf16[6144,512]{1,0:T(8,128)(2,1)} %param.9), kind=kLoop, calls=%fused_computation.31 | loop fusion | flops 12570624 | bytes 6340608 | tf_op jit(solution)/shard_map/reduce_sum | solution.py:15
  12.1 8.0 %multiply_convert_fusion = bf16[6144,512]{0,1:T(8,128)(2,1)S(1)} fusion(bf16[512,512]{1,0:T(8,128)(2,1)S(1)} %copy-done, bf16[6144,512]{1,0:T(8,128)(2,1)S(1)} %copy-done.2, f32[6144]{0:T(1024)S(1)} %get-tuple-element.106, f32[6144]{0:T(1024)S(1)} %get-tuple-element.105), kind=kOutput, calls=%fused_computation.28 | convolution fusion | flops 3249537024 | bytes 13156352 | tf_op jit(solution)/shard_map/dot_general | solution.py:62
  23.6 2.6 copy.28
  28.8 2.8 concatenate.10
  34.6 74.4 %while.11 = (s32[]{:T(128)}, f32[12,512,128]{2,1,0:T(8,128)}, s32[12]{0:T(128)S(1)}, s32[6144]{0:T(1024)S(1)}, s32[6272]{0:T(1024)S(1)}, /*index=5*/bf16[6144,12...) while((s32[]{:T(128)}, f32[12,512,128]{2,1,0:T(8,128)}, ...), condition=%wide.region_10.11_spmd.clone, body=%wide.region_9.10_spmd.clone.sunk | while | flops 171377152 | bytes 741060 | solution.py:50
  56.8 2.6 fusion.65
  63.0 2.6 fusion.65
  69.2 2.6 fusion.65
  81.6 2.6 fusion.65
  87.8 2.6 fusion.65
  106.4 2.6 fusion.65
  109.0 3.6 %fusion.55 = (f32[12,512]{1,0:T(8,128)S(1)}, f32[12,512]{1,0:T(8,128)S(1)}) fusion(f32[12,512,128]{2,1,0:T(8,128)} %get-tuple-element.54), kind=kLoop, calls=%fused_computation.120 | loop fusion | flops 2347008 | bytes 3194880 | tf_op jit(solution)/shard_map/reduce_sum | solution.py:67
  112.6 3.6 %copy.25 = f32[6144,128]{0,1:T(8,128)} copy(f32[6144,128]{1,0:T(8,128)} %bitcast.66) | data formatting | bytes 6291456 | tf_op jit(solution)/shard_map/reshape | solution.py:50
  116.2 13.3 %all-reduce.3 = (f32[6144]{0:T(1024)S(1)}, f32[6144]{0:T(1024)S(1)}) all-reduce(f32[6144]{0:T(1024)S(1)} %reduce_sum.119, f32[6144]{0:T(1024)S(1)} %reduce_sum.117), channel_id=1, replica_groups=mesh['dp'=8,'mp'=4] {'mp'}, use_global_device_ids=true, to_apply=%region_14.15 | all-reduce | flops 12288 | bytes 98304 | tf_op jit(solution)/shard_map/psum | solution.py:67
  129.5 8.8 %fusion.30 = f32[6144,512]{1,0:T(8,128)} fusion(f32[6144,128]{0,1:T(8,128)} %copy.25, bf16[6144,1,4,128]{0,3,2,1:T(8,128)(2,1)} %bitcast.68, f32[6144]{0:T(1024)S(1)} %get-tuple-element.104, f32[6144]{0:T(1024)S(1)} %get-tuple-element.103, bf16[512,512]{1,0:T(8,128)(2,1)} %param.11, s32[]{:T(128)S(6)} %select_n.164), kind=kOutput, calls=%fused_computation.39 | convolution fusion | flops 809238528 | bytes 17481732 | tf_op jit(solution)/shard_map/dot_general | solution.py:77
  138.3 12.2 %convert_element_type.24 = f32[6144,512]{1,0:T(8,128)} convert(bf16[6144,512]{1,0:T(8,128)(2,1)} %param.9) | non-fusion elementwise | flops 3145728 | bytes 18874368 | tf_op jit(solution)/shard_map/convert_element_type | solution.py:60
  151.2 20.7 %all-gather.2 = s32[8,1,24]{2,1,0:T(1,128)S(1)} all-gather(s32[1,1,24]{2,1,0:T(1,128)S(1)} %bitcast.82), channel_id=1, replica_groups=mesh['dp'=8,'mp'=4] {'dp'}, dimensions={0}, use_global_device_ids=true | all-gather | bytes 864 | tf_op jit(solution)/shard_map/all_gather | solution.py:116
  171.9 64.0 %reduce-scatter.2.cloned.1.call-done = f32[6144,128]{1,0:T(8,128)} async-done(((f32[6144,512]{1,0:T(8,128)}), f32[6144,128]{1,0:T(8,128)}) %reduce-scatter.2.cloned.1.call-update) | async-done | bytes 3145744 | tf_op jit(solution)/shard_map/reduce_scatter | solution.py:78
  235.9 3.2 add_convert_fusion
  241.0 2.8 broadcast_select_fusion
  243.8 5.7 %all-to-all-start = ((bf16[8,6,128,128]{3,2,1,0:T(8,128)(2,1)}), bf16[8,6,128,128]{3,2,1,0:T(8,128)(2,1)}, u32[]{:S(2)}, u32[]{:S(2)}) async-start(bf16[8,6,128,128]{3,2,1,0:T(8,128)(2,1)} %broadcast_select_fusion), calls=%async_computation.1 | async-start | bytes 3145728 | tf_op jit(solution)/shard_map/all_to_all | solution.py:153
  250.7 39.2 %all-gather = s32[8,1,24]{2,1,0:T(1,128)S(1)} all-gather(s32[1,1,24]{2,1,0:T(1,128)S(1)} %bitcast.80), channel_id=1, replica_groups=mesh['dp'=8,'mp'=4] {'dp'}, dimensions={0}, use_global_device_ids=true | all-gather | bytes 864 | tf_op jit(solution)/shard_map/all_gather | solution.py:117
  290.5 23.1 %all-gather.1 = s32[8,1,24]{2,1,0:T(1,128)S(1)} all-gather(s32[1,1,24]{2,1,0:T(1,128)S(1)} %bitcast.85), channel_id=1, replica_groups=mesh['dp'=8,'mp'=4] {'dp'}, dimensions={0}, use_global_device_ids=true | all-gather | bytes 864 | tf_op jit(solution)/shard_map/all_gather | solution.py:118
  318.2 5.2 %fusion.32 = bf16[6144,128]{1,0:T(8,128)(2,1)} fusion(bf16[48,128,128]{2,1,0:T(8,128)(2,1)S(1)} %gather_fusion.1, pred[6144]{0:T(1024)(128)(4,1)S(1)} %get-tuple-element.114, pred[6144]{0:T(1024)(128)(4,1)S(1)} %get-tuple-element.113), kind=kLoop, calls=%fused_computation.42 | loop fusion | flops 1572864 | bytes 3158016 | tf_op jit(solution)/shard_map/jit(_where)/select_n | solution.py:157
  (126 shorter events, 42.7 us)
Async XLA Ops:
  7.2 4.9 %copy-start = (bf16[512,512]{1,0:T(8,128)(2,1)S(1)}, bf16[512,512]{1,0:T(8,128)(2,1)}, u32[]{:S(2)}) copy-start(bf16[512,512]{1,0:T(8,128)(2,1)} %param.10) | copy-start | bytes 1572868
  7.2 228.7 %reduce-scatter.2.cloned.1.call-start = ((), (), s32[]{:S(2)}) async-start(), calls=%async_computation.2 | async-start | bytes 15728640 | tf_op jit(solution)/shard_map/reduce_scatter | solution.py:78
  7.2 4.8 %copy-start.2 = (bf16[6144,512]{1,0:T(8,128)(2,1)S(1)}, bf16[6144,512]{1,0:T(8,128)(2,1)}, u32[]{:S(2)}) copy-start(bf16[6144,512]{1,0:T(8,128)(2,1)} %param.9) | copy-start | bytes 18874372
  20.1 3.5 %copy-start.3 = (bf16[6144,512]{0,1:T(8,128)(2,1)}, bf16[6144,512]{0,1:T(8,128)(2,1)S(1)}, u32[]{:S(2)}) copy-start(bf16[6144,512]{0,1:T(8,128)(2,1)S(1)} %multiply_convert_fusion) | copy-start | bytes 18874372
  28.8 2.8 copy-start.4
  32.8 1.6 copy-start.6
  32.8 1.6 copy-start.7
  138.3 12.2 %copy-start.5 = (s32[1,24]{1,0:T(1,128)S(1)}, s32[1,24]{1,0:T(1,128)}, u32[]{:S(2)}) copy-start(s32[1,24]{1,0:T(1,128)} %param.13) | copy-start | bytes 292
  243.8 46.7 %copy-start.8 = (s32[1,24]{1,0:T(1,128)S(1)}, s32[1,24]{1,0:T(1,128)}, u32[]{:S(2)}) copy-start(s32[1,24]{1,0:T(1,128)} %param.14) | copy-start | bytes 292
  243.8 72.1 %all-to-all-start = ((bf16[8,6,128,128]{3,2,1,0:T(8,128)(2,1)}), bf16[8,6,128,128]{3,2,1,0:T(8,128)(2,1)}, u32[]{:S(2)}, u32[]{:S(2)}) async-start(bf16[8,6,128,128]{3,2,1,0:T(8,128)(2,1)} %broadcast_select_fusion), calls=%async_computation.1 | async-start | bytes 3145728 | tf_op jit(solution)/shard_map/all_to_all | solution.py:153
  315.9 7.6 %copy-start.1 = (bf16[512,512]{1,0:T(8,128)(2,1)S(1)}, bf16[512,512]{1,0:T(8,128)(2,1)}, u32[]{:S(2)}) copy-start(bf16[512,512]{1,0:T(8,128)(2,1)} %param.10) | copy-start | bytes 1572868
Sparse Core Ops, SparseCore 0:
  138.4 97.4 reduce-scatter.1
where the time goes:
time: 331 us; the launch traced here: 330 us
  blocking collectives  96.2 us (29%)
  waiting for transfers between devices  64.1 us (19%)
  matrix products  48.1 us (15%)
  other arithmetic  34.9 us (11%)
  loops' own time  34.2 us (10%)
  local copies, waits for them, and re-layouts  32.8 us (10%)
  between operations  14.3 us (4%)
  starting transfers between devices  5.7 us (2%)
    reduce_scatter x1, waiting for transfers between devices, layer_rows(): lax.psum_scatter(partial_term, 'mp', scatter_dimension=1, tiled=True)  64 us
    all_gather x1, blocking collectives, per_device(): lax.all_gather(owner, 'dp', axis=0, tiled=True)  39.2 us
    another operation x1, loops' own time, attend(): return lax.map(one_tile, tile_starts).reshape(row_count, head_size)  34.2 us
    dot_general x12, matrix products, one_tile(): return jnp.dot(weights, value_tile, preferred_element_type=jnp.float32)  31.4 us
    all_gather x1, blocking collectives, per_device(): lax.all_gather(recv_offset, 'dp', axis=0, tiled=True)  23.1 us
    all_gather x1, blocking collectives, per_device(): lax.all_gather(hist_len, 'dp', axis=0, tiled=True)  20.7 us
    psum x1, blocking collectives, layer_rows(): lax.psum((jnp.sum(outputs, 1), jnp.sum(outputs * outputs, 1)), 'mp')  13.3 us
    convert_element_type x1, other arithmetic, layer_rows(): widened = rows_in.astype(jnp.float32)  12.2 us
  transfers between devices with their start and end apart: 2, of which 1 were waited for; matrix products, arithmetic and copies ran while one was open for 5% of the time, Pallas kernels for 0%

commit v1 on v0

--- a/solution.py
+++ b/solution.py
@@ -115,7 +115,12 @@
     all_len, all_owner, all_offset = (
         lax.all_gather(hist_len, "dp", axis=0, tiled=True),
         lax.all_gather(owner, "dp", axis=0, tiled=True),
-        lax.all_gather(recv_offset, "dp", axis=0, tiled=True),
+        jnp.concatenate(
+            lax.all_to_all(
+                jnp.stack([recv_offset for _ in range(lax.psum(1, "dp"))], axis=0), "dp", 0, 0
+            ),
+            axis=0,
+        ),
     )
     all_counts = (all_len + BLOCK - 1) // BLOCK
     all_before = (all_owner[:, :, None] == all_owner[:, None, :]) & earlier[None]

time: 331 us -> 311 us (0.940)
  blocking collectives: 96.2 us -> 73.6 us
  waiting for transfers between devices: 64.1 us -> 56.3 us
  starting transfers between devices: 5.7 us -> 11.4 us
    all_gather x1 -> x0, blocking collectives: 23.1 us -> none  [per_device(): lax.all_gather(recv_offset, 'dp', axis=0, tiled=True)]
    reduce_scatter x1, waiting for transfers between devices: 64 us -> 56.3 us  [layer_rows(): lax.psum_scatter(partial_term, 'mp', scatter_dimension=1, tiled=True)]
    all_to_all x0 -> x1, starting transfers between devices: none -> 5.82 us  [per_device(): lax.all_to_all(jnp.stack([recv_offset for _ in range(lax.psum(1, 'dp'))],...]
  transfers between devices with their start and end apart: 2 -> 3, of which waited for: 1 -> 1; matrix products, arithmetic and copies ran while one was open for 5% -> 8% of each run, Pallas kernels for 0% -> 0%
where the time goes in v1:
time: 311 us; the launch traced here: 307 us
  blocking collectives  73.6 us (24%)
  waiting for transfers between devices  56.3 us (18%)
  matrix products  48.1 us (15%)
  other arithmetic  35.2 us (11%)
  loops' own time  34.2 us (11%)
  local copies, waits for them, and re-layouts  34 us (11%)
  between operations  14.3 us (5%)
  starting transfers between devices  11.4 us (4%)
    reduce_scatter x1, waiting for transfers between devices, layer_rows(): lax.psum_scatter(partial_term, 'mp', scatter_dimension=1, tiled=True)  56.3 us
    all_gather x1, blocking collectives, per_device(): lax.all_gather(owner, 'dp', axis=0, tiled=True)  39.2 us
    another operation x1, loops' own time, attend(): return lax.map(one_tile, tile_starts).reshape(row_count, head_size)  34.2 us
    dot_general x12, matrix products, one_tile(): return jnp.dot(weights, value_tile, preferred_element_type=jnp.float32)  31.4 us
    all_gather x1, blocking collectives, per_device(): lax.all_gather(hist_len, 'dp', axis=0, tiled=True)  21.1 us
    psum x1, blocking collectives, layer_rows(): lax.psum((jnp.sum(outputs, 1), jnp.sum(outputs * outputs, 1)), 'mp')  13.3 us
    convert_element_type x1, other arithmetic, layer_rows(): widened = rows_in.astype(jnp.float32)  12.4 us
    dot_general x1, matrix products, layer_rows(): jnp.dot(gated_rows, own_rows, preferred_element_type=jnp.float32)  8.77 us
  transfers between devices with their start and end apart: 3, of which 1 were waited for; matrix products, arithmetic and copies ran while one was open for 8% of the time, Pallas kernels for 0%

profile of v1, /device:TPU:0, one launch (start us, length us, event | category | flops | bytes accessed | tf_op | source)
XLA Modules:
  0.0 307.1 jit_solution(4211578608511765427)
XLA Ops:
  7.3 4.8 %convert_reduce_fusion = (f32[6144]{0:T(1024)S(1)}, f32[6144]{0:T(1024)S(1)}) fusion(bf16[6144,512]{1,0:T(8,128)(2,1)} %param.9), kind=kLoop, calls=%fused_computation.31 | loop fusion | flops 12570624 | bytes 6340608 | tf_op jit(solution)/shard_map/reduce_sum | solution.py:15
  12.1 8.0 %multiply_convert_fusion = bf16[6144,512]{0,1:T(8,128)(2,1)S(1)} fusion(bf16[512,512]{1,0:T(8,128)(2,1)S(1)} %copy-done, bf16[6144,512]{1,0:T(8,128)(2,1)S(1)} %copy-done.2, f32[6144]{0:T(1024)S(1)} %get-tuple-element.106, f32[6144]{0:T(1024)S(1)} %get-tuple-element.105), kind=kOutput, calls=%fused_computation.28 | convolution fusion | flops 3249537024 | bytes 13156352 | tf_op jit(solution)/shard_map/dot_general | solution.py:62
  23.6 2.6 copy.28
  28.8 2.8 concatenate.10
  34.6 74.4 %while.11 = (s32[]{:T(128)}, f32[12,512,128]{2,1,0:T(8,128)}, s32[12]{0:T(128)S(1)}, s32[6144]{0:T(1024)S(1)}, s32[6272]{0:T(1024)S(1)}, /*index=5*/bf16[6144,12...) while((s32[]{:T(128)}, f32[12,512,128]{2,1,0:T(8,128)}, ...), condition=%wide.region_10.11_spmd.clone, body=%wide.region_9.10_spmd.clone.sunk | while | flops 171377152 | bytes 741060 | solution.py:50
  56.8 2.6 fusion.65
  63.0 2.6 fusion.65
  69.2 2.6 fusion.65
  81.6 2.6 fusion.65
  87.8 2.6 fusion.65
  106.4 2.6 fusion.65
  109.0 3.6 %fusion.55 = (f32[12,512]{1,0:T(8,128)S(1)}, f32[12,512]{1,0:T(8,128)S(1)}) fusion(f32[12,512,128]{2,1,0:T(8,128)} %get-tuple-element.54), kind=kLoop, calls=%fused_computation.120 | loop fusion | flops 2347008 | bytes 3194880 | tf_op jit(solution)/shard_map/reduce_sum | solution.py:67
  112.6 3.6 %copy.25 = f32[6144,128]{0,1:T(8,128)} copy(f32[6144,128]{1,0:T(8,128)} %bitcast.66) | data formatting | bytes 6291456 | tf_op jit(solution)/shard_map/reshape | solution.py:50
  116.2 13.3 %all-reduce.3 = (f32[6144]{0:T(1024)S(1)}, f32[6144]{0:T(1024)S(1)}) all-reduce(f32[6144]{0:T(1024)S(1)} %reduce_sum.119, f32[6144]{0:T(1024)S(1)} %reduce_sum.117), channel_id=1, replica_groups=mesh['dp'=8,'mp'=4] {'mp'}, use_global_device_ids=true, to_apply=%region_14.15 | all-reduce | flops 12288 | bytes 98304 | tf_op jit(solution)/shard_map/psum | solution.py:67
  129.5 8.8 %fusion.30 = f32[6144,512]{1,0:T(8,128)} fusion(f32[6144,128]{0,1:T(8,128)} %copy.25, bf16[6144,1,4,128]{0,3,2,1:T(8,128)(2,1)} %bitcast.68, f32[6144]{0:T(1024)S(1)} %get-tuple-element.104, f32[6144]{0:T(1024)S(1)} %get-tuple-element.103, bf16[512,512]{1,0:T(8,128)(2,1)} %param.11, s32[]{:T(128)S(6)} %select_n.164), kind=kOutput, calls=%fused_computation.39 | convolution fusion | flops 809238528 | bytes 17481732 | tf_op jit(solution)/shard_map/dot_general | solution.py:77
  139.6 5.8 %all-to-all-start = ((s32[8,1,24]{2,1,0:T(1,128)}), s32[8,1,24]{2,1,0:T(1,128)S(1)}, u32[]{:S(2)}, u32[]{:S(2)}) async-start(s32[8,1,24]{2,1,0:T(1,128)} %stack.2), calls=%async_computation | async-start | bytes 8192 | tf_op jit(solution)/shard_map/all_to_all | solution.py:119
  145.4 12.4 %convert_element_type.24 = f32[6144,512]{1,0:T(8,128)} convert(bf16[6144,512]{1,0:T(8,128)(2,1)} %param.9) | non-fusion elementwise | flops 3145728 | bytes 18874368 | tf_op jit(solution)/shard_map/convert_element_type | solution.py:60
  158.5 21.1 %all-gather.1 = s32[8,1,24]{2,1,0:T(1,128)S(1)} all-gather(s32[1,1,24]{2,1,0:T(1,128)S(1)} %bitcast.82), channel_id=1, replica_groups=mesh['dp'=8,'mp'=4] {'dp'}, dimensions={0}, use_global_device_ids=true | all-gather | bytes 864 | tf_op jit(solution)/shard_map/all_gather | solution.py:116
  179.7 56.3 %reduce-scatter.2.cloned.1.call-done = f32[6144,128]{1,0:T(8,128)} async-done(((f32[6144,512]{1,0:T(8,128)}), f32[6144,128]{1,0:T(8,128)}) %reduce-scatter.2.cloned.1.call-update) | async-done | bytes 3145744 | tf_op jit(solution)/shard_map/reduce_scatter | solution.py:78
  235.9 3.2 %add_convert_fusion = bf16[6144,128]{1,0:T(8,128)(2,1)S(1)} fusion(f32[6144,128]{1,0:T(8,128)} %reduce-scatter.2.cloned.1.call-done, f32[6144,512]{1,0:T(8,128)} %convert_element_type.24, s32[]{:T(128)S(6)} %select_n.164), kind=kLoop, calls=%fused_computation.37 | loop fusion | flops 1572864 | bytes 7864324 | tf_op jit(solution)/shard_map/convert_element_type | solution.py:80
  241.0 2.8 broadcast_select_fusion
  243.8 5.5 %all-to-all-start.1 = ((bf16[8,6,128,128]{3,2,1,0:T(8,128)(2,1)}), bf16[8,6,128,128]{3,2,1,0:T(8,128)(2,1)}, u32[]{:S(2)}, u32[]{:S(2)}) async-start(bf16[8,6,128,128]{3,2,1,0:T(8,128)(2,1)} %broadcast_select_fusion), calls=%async_computation.2 | async-start | bytes 3145728 | tf_op jit(solution)/shard_map/all_to_all | solution.py:158
  250.6 39.2 %all-gather = s32[8,1,24]{2,1,0:T(1,128)S(1)} all-gather(s32[1,1,24]{2,1,0:T(1,128)S(1)} %bitcast.80), channel_id=1, replica_groups=mesh['dp'=8,'mp'=4] {'dp'}, dimensions={0}, use_global_device_ids=true | all-gather | bytes 864 | tf_op jit(solution)/shard_map/all_gather | solution.py:117
  295.0 5.2 %fusion.32 = bf16[6144,128]{1,0:T(8,128)(2,1)} fusion(bf16[48,128,128]{2,1,0:T(8,128)(2,1)S(1)} %gather_fusion.1, pred[6144]{0:T(1024)(128)(4,1)S(1)} %get-tuple-element.114, pred[6144]{0:T(1024)(128)(4,1)S(1)} %get-tuple-element.113), kind=kLoop, calls=%fused_computation.42 | loop fusion | flops 1572864 | bytes 3158016 | tf_op jit(solution)/shard_map/jit(_where)/select_n | solution.py:162
  (128 shorter events, 44.0 us)
Async XLA Ops:
  7.2 4.9 %copy-start = (bf16[512,512]{1,0:T(8,128)(2,1)S(1)}, bf16[512,512]{1,0:T(8,128)(2,1)}, u32[]{:S(2)}) copy-start(bf16[512,512]{1,0:T(8,128)(2,1)} %param.10) | copy-start | bytes 1572868
  7.2 228.7 %reduce-scatter.2.cloned.1.call-start = ((), (), s32[]{:S(2)}) async-start(), calls=%async_computation.3 | async-start | bytes 15728640 | tf_op jit(solution)/shard_map/reduce_scatter | solution.py:78
  7.2 4.8 %copy-start.2 = (bf16[6144,512]{1,0:T(8,128)(2,1)S(1)}, bf16[6144,512]{1,0:T(8,128)(2,1)}, u32[]{:S(2)}) copy-start(bf16[6144,512]{1,0:T(8,128)(2,1)} %param.9) | copy-start | bytes 18874372
  20.0 3.5 %copy-start.3 = (bf16[6144,512]{0,1:T(8,128)(2,1)}, bf16[6144,512]{0,1:T(8,128)(2,1)S(1)}, u32[]{:S(2)}) copy-start(bf16[6144,512]{0,1:T(8,128)(2,1)S(1)} %multiply_convert_fusion) | copy-start | bytes 18874372
  28.8 2.8 copy-start.4
  32.8 1.6 copy-start.6
  32.8 1.6 copy-start.7
  138.3 0.7 copy-start.8
  139.6 104.2 %all-to-all-start = ((s32[8,1,24]{2,1,0:T(1,128)}), s32[8,1,24]{2,1,0:T(1,128)S(1)}, u32[]{:S(2)}, u32[]{:S(2)}) async-start(s32[8,1,24]{2,1,0:T(1,128)} %stack.2), calls=%async_computation | async-start | bytes 8192 | tf_op jit(solution)/shard_map/all_to_all | solution.py:119
  145.4 12.5 %copy-start.5 = (s32[1,24]{1,0:T(1,128)S(1)}, s32[1,24]{1,0:T(1,128)}, u32[]{:S(2)}) copy-start(s32[1,24]{1,0:T(1,128)} %param.13) | copy-start | bytes 292
  243.8 48.9 %all-to-all-start.1 = ((bf16[8,6,128,128]{3,2,1,0:T(8,128)(2,1)}), bf16[8,6,128,128]{3,2,1,0:T(8,128)(2,1)}, u32[]{:S(2)}, u32[]{:S(2)}) async-start(bf16[8,6,128,128]{3,2,1,0:T(8,128)(2,1)} %broadcast_select_fusion), calls=%async_computation.2 | async-start | bytes 3145728 | tf_op jit(solution)/shard_map/all_to_all | solution.py:158
  292.7 7.6 %copy-start.1 = (bf16[512,512]{1,0:T(8,128)(2,1)S(1)}, bf16[512,512]{1,0:T(8,128)(2,1)}, u32[]{:S(2)}) copy-start(bf16[512,512]{1,0:T(8,128)(2,1)} %param.10) | copy-start | bytes 1572868
Sparse Core Ops, SparseCore 0:
  138.4 97.4 reduce-scatter.1
